TPU v7x, 512 devices: a whole 4x8x8 slice. The times are simulated.
512 devices in a mesh: dp: 256 (over x, y, z), outer: 2 (over core).
Axes of the slice: x: 4, y: 8, z: 8, core: 2. Of those that a mesh axis runs over, the one named last changes fastest.
Arguments:
- gradient: float32 [512, 131072], P(('dp', 'outer')), may hold values from -6 to 6
- residual: float32 [512, 131072], P(('dp', 'outer')), may hold values from -6 to 6
- indices: int32 [512, 512], P(('dp', 'outer')), may hold values from 0 to 131071, as said below
- params: float32 [131072], replicated, may hold values from -6 to 6
Outputs:
- new_params: float32 [131072], replicated
- new_residual: float32 [512, 131072], P(('dp', 'outer'))
Inputs may be any that keep to these rules, and one draw needn't show every extreme that they name: Within each worker's row the 512 indices are distinct and increasing: index j lies in [j * 256, (j + 1) * 256). Different workers often pick the same coordinate.
All inputs are finite; a program needn't handle non-finite values.
Results may differ from a plain program's by a relative error of at most 0.0003.
Values sent between devices are 32-bit elements.
No kernel may reach another device: no remote copies, remote signals or barrier semaphores. Data moves between devices by JAX's collectives and lax.ppermute only.
A program may use at most 64 MiB of HBM per device.

v0:
```python
import jax
import jax.numpy as jnp
from jax import lax
from jax.sharding import Mesh
from jax.sharding import PartitionSpec as P

DP_OUTER = ("dp_0", "dp_1", "dp_2", "outer")
step_size = 0.5


def split_up(array, dim, devices):
    return jnp.stack(jnp.split(array, devices, axis=dim))


def scatter_pairs(array, chips, core, dim):
    sizes = (lax.axis_size(chips), lax.axis_size(core))
    parts = split_up(array, dim, sizes[0] * sizes[1])
    inside = parts.shape[1:]
    parts = parts.reshape(*sizes, *inside).swapaxes(0, 1).reshape(-1, *inside)
    parts = lax.psum_scatter(parts, core, scatter_dimension=0, tiled=True)
    return lax.psum_scatter(parts, chips, scatter_dimension=0, tiled=True)[0]


def shards(gradient, residual, indices, params):
    accumulated = gradient[0] + residual[0]
    positions = indices[0]
    values_sent = accumulated[positions]
    new_residual = accumulated.at[positions].set(jnp.float32(0.0))[None, :]
    empty = jnp.zeros((accumulated.shape[0],), jnp.float32)
    spread = empty.at[positions].add(values_sent)
    portion = scatter_pairs(spread, ("dp_0", "dp_1", "dp_2"), "outer", 0)
    length = portion.shape[0]
    first = lax.axis_index(DP_OUTER) * length
    own_params = lax.dynamic_slice_in_dim(params, first, length)
    updated = own_params - step_size * portion
    new_params = lax.all_gather(updated, DP_OUTER, axis=0, tiled=True)
    return (new_params, new_residual)


def solution(mesh):
    torus = Mesh(
        mesh.devices.reshape(4, 8, 8, mesh.shape["outer"]), ("dp_0", "dp_1", "dp_2", "outer")
    )
    placed = (P(DP_OUTER, None), P(DP_OUTER, None), P(DP_OUTER, None), P())
    return jax.shard_map(
        shards, mesh=torus, in_specs=placed, out_specs=(P(), P(DP_OUTER, None)), check_vma=False
    )
```

profile of v0, /device:TPU:1, one launch (start us, length us, event | category | flops | bytes accessed | tf_op | source)
XLA Modules:
  0.0 359.0 jit_solution(5409333906929286416)
XLA Ops:
  7.2 0.0 reduce-scatter.2.cloned.1.call-start
  7.2 0.7 compare_select_fusion
  7.9 1.7 add.41
  9.7 3.1 gather_fusion
  12.8 3.7 %scatter_custom_fusion = f32[131072]{0:T(1024)S(1)} fusion(s32[512]{0:T(512)S(1)} %bitcast.530, f32[512]{0:T(512)S(1)} %gather_fusion, f32[]{:T(128)} %constant.34.clone.1), kind=kCustom, calls=%fused_computation.4 | custom fusion | flops 512 | bytes 524292 | tf_op jit(solution)/shard_map/scatter-add | solution.py:30
  17.0 0.8 concatenate
  17.9 0.8 concatenate.1
  18.7 0.3 reshape.41
  19.0 0.8 copy.7
  19.9 0.0 reduce-scatter.2.cloned.1.call-update
  19.9 0.0 all-reduce.3.cloned.1.call-start
  19.9 23.1 %reduce-scatter.2.cloned.1.call-done = f32[256,256]{1,0:T(8,128)} async-done(((f32[512,256]{1,0:T(8,128)}), f32[256,256]{1,0:T(8,128)}) %reduce-scatter.2.cloned.1.call-update) | async-done | bytes 262160 | tf_op jit(solution)/shard_map/reduce_scatter | solution.py:20
  43.0 0.0 all-reduce.3.cloned.1.call-update
  43.1 2.7 scatter_fusion
  45.8 0.0 copy-start
  45.8 1.3 dynamic-slice
  47.1 230.3 %all-reduce.3.cloned.1.call-done = f32[256,256]{1,0:T(8,128)} async-done(((f32[256,256]{1,0:T(8,128)}), f32[256,256]{1,0:T(8,128)}) %all-reduce.3.cloned.1.call-update) | async-done | bytes 262160
  277.4 1.3 dynamic-slice_multiply_fusion
  278.8 0.8 dynamic-slice_subtract_fusion
  279.6 71.8 %all-gather = f32[512,1,256]{2,1,0:T(1,128)S(1)} all-gather(f32[1,1,256]{2,1,0:T(1,128)S(1)} %bitcast.1044), channel_id=1, replica_groups=mesh['dp_0'=4,'dp_1'=8,'dp_2'=8,'outer'=2] {'dp_0','dp_1','dp_2','outer'}, dimensions={0}, use_global_device_ids=true | all-gather | bytes 525312 | tf_op jit(solution)/shard_map/all_gather | solution.py:36
  351.4 0.8 copy.11
  352.2 0.0 copy-done
  (31 shorter events, 0.4 us)
Async XLA Ops:
  7.2 35.9 %reduce-scatter.2.cloned.1.call-start = ((), (), s32[]{:S(2)}) async-start(), calls=%async_computation.1 | async-start | bytes 786432 | tf_op jit(solution)/shard_map/reduce_scatter | solution.py:20
  19.9 257.5 %all-reduce.3.cloned.1.call-start = ((), (), s32[]{:S(2)}) async-start(), calls=%async_computation.2 | async-start | bytes 524288
  45.8 306.4 %copy-start = (f32[131072]{0:T(1024)}, f32[131072]{0:T(1024)S(1)}, u32[]{:S(2)}) copy-start(f32[131072]{0:T(1024)S(1)} %scatter_fusion) | copy-start | bytes 1572868
Sparse Core Ops, SparseCore 0:
  20.0 22.9 reduce-scatter.1
  48.0 229.4 all-reduce.2
where the time goes:
time: 359 us
  waiting for transfers between devices  253 us (70%)
  blocking collectives  71.8 us (20%)
  between operations  14.3 us (4%)
  local copies, waits for them, and re-layouts  11.1 us (3%)
  other arithmetic  8.24 us (2%)
    unnamed x3, waiting for transfers between devices  230 us
    all_gather x1, blocking collectives, shards(): new_params = lax.all_gather(updated, DP_OUTER, axis=0, tiled=True)  71.8 us
    reduce_scatter x1, waiting for transfers between devices, scatter_pairs(): parts = lax.psum_scatter(parts, core, scatter_dimension=0, tiled=True)  23.1 us
  transfers between devices with their start and end apart: 2, of which 2 were waited for; matrix products, arithmetic and copies ran while one was open for 1% of the time, Pallas kernels for 0%

commit v1 on v0

--- a/solution.py
+++ b/solution.py
@@ -1,3 +1,4 @@
+import functools
 import jax
 import jax.numpy as jnp
 from jax import lax
@@ -6,6 +7,16 @@
 
 DP_OUTER = ("dp_0", "dp_1", "dp_2", "outer")
 step_size = 0.5
+
+
+def record_enter(arr_in, along_axis):
+    piece_now = lax.axis_size(along_axis)
+    local_out = jnp.stack([arr_in] * piece_now)
+    tmp = lax.all_to_all(local_out, along_axis, 0, 0)
+    return jnp.concatenate(tmp, axis=0)
+
+
+register_local_data = functools.partial(record_enter, along_axis=DP_OUTER)
 
 
 def split_up(array, dim, devices):
@@ -33,7 +44,7 @@
     first = lax.axis_index(DP_OUTER) * length
     own_params = lax.dynamic_slice_in_dim(params, first, length)
     updated = own_params - step_size * portion
-    new_params = lax.all_gather(updated, DP_OUTER, axis=0, tiled=True)
+    new_params = register_local_data(updated)
     return (new_params, new_residual)
 
 

time: 359 us -> 327 us (0.911)
  blocking collectives: 71.8 us -> 0 us
  waiting for transfers between devices: 253 us -> 275 us
  starting transfers between devices: 0.08 us -> 17.1 us
    all_gather x1 -> x0, blocking collectives: 71.8 us -> none  [shards(): new_params = lax.all_gather(updated, DP_OUTER, axis=0, tiled=True)]
    all_to_all x0 -> x1, waiting for transfers between devices: none -> 19.1 us  [record_enter(): tmp = lax.all_to_all(local_out, along_axis, 0, 0)]
    all_to_all x0 -> x1, starting transfers between devices: none -> 17.1 us  [record_enter(): tmp = lax.all_to_all(local_out, along_axis, 0, 0)]
  transfers between devices with their start and end apart: 2 -> 3, of which waited for: 2 -> 3; matrix products, arithmetic and copies ran while one was open for 1% -> 1% of each run, Pallas kernels for 0% -> 0%
where the time goes in v1:
time: 327 us
  waiting for transfers between devices  275 us (84%)
  starting transfers between devices  17.1 us (5%)
  between operations  14.3 us (4%)
  local copies, waits for them, and re-layouts  12.1 us (4%)
  other arithmetic  8.24 us (3%)
    unnamed x3, waiting for transfers between devices  233 us
    reduce_scatter x1, waiting for transfers between devices, scatter_pairs(): parts = lax.psum_scatter(parts, core, scatter_dimension=0, tiled=True)  23.1 us
    all_to_all x1, waiting for transfers between devices, record_enter(): tmp = lax.all_to_all(local_out, along_axis, 0, 0)  19.1 us
    all_to_all x1, starting transfers between devices, record_enter(): tmp = lax.all_to_all(local_out, along_axis, 0, 0)  17.1 us
  transfers between devices with their start and end apart: 3, of which 3 were waited for; matrix products, arithmetic and copies ran while one was open for 1% of the time, Pallas kernels for 0%

profile of v1, /device:TPU:1, one launch (start us, length us, event | category | flops | bytes accessed | tf_op | source)
XLA Modules:
  0.0 327.2 jit_solution(6292188392576828960)
XLA Ops:
  7.2 0.0 reduce-scatter.2.cloned.1.call-start
  7.2 0.7 compare_select_fusion
  7.9 1.7 add.41
  9.7 3.1 gather_fusion
  12.8 3.7 %scatter_custom_fusion = f32[131072]{0:T(1024)S(1)} fusion(s32[512]{0:T(512)S(1)} %bitcast.529, f32[512]{0:T(512)S(1)} %gather_fusion, f32[]{:T(128)} %constant.34.clone.1), kind=kCustom, calls=%fused_computation.4 | custom fusion | flops 512 | bytes 524292 | tf_op jit(solution)/shard_map/scatter-add | solution.py:41
  17.0 0.8 concatenate
  17.9 0.8 concatenate.1
  18.7 0.3 reshape.52
  19.0 0.8 copy.7
  19.9 0.0 reduce-scatter.2.cloned.1.call-update
  19.9 0.0 all-reduce.3.cloned.1.call-start
  19.9 23.1 %reduce-scatter.2.cloned.1.call-done = f32[256,256]{1,0:T(8,128)} async-done(((f32[512,256]{1,0:T(8,128)}), f32[256,256]{1,0:T(8,128)}) %reduce-scatter.2.cloned.1.call-update) | async-done | bytes 262160 | tf_op jit(solution)/shard_map/reduce_scatter | solution.py:31
  43.0 0.0 all-reduce.3.cloned.1.call-update
  43.1 1.3 dynamic-slice
  44.3 233.1 %all-reduce.3.cloned.1.call-done = f32[256,256]{1,0:T(8,128)} async-done(((f32[256,256]{1,0:T(8,128)}), f32[256,256]{1,0:T(8,128)}) %all-reduce.3.cloned.1.call-update) | async-done | bytes 262160
  277.4 1.3 dynamic-slice_multiply_fusion
  278.8 0.8 dynamic-slice_subtract_fusion
  279.6 1.1 stack.2567
  280.6 17.1 %all-to-all-start = ((f32[512,1,256]{2,1,0:T(1,128)}), f32[512,1,256]{2,1,0:T(1,128)S(1)}, u32[]{:S(2)}, u32[]{:S(2)}) async-start(f32[512,1,256]{2,1,0:T(1,128)} %stack.2567), calls=%async_computation.1 | async-start | bytes 1048576 | tf_op jit(solution)/shard_map/all_to_all | solution.py:15
  297.7 2.7 scatter_fusion
  300.4 0.0 copy-start
  300.4 19.1 %all-to-all-done = f32[512,1,256]{2,1,0:T(1,128)S(1)} async-done(((f32[512,1,256]{2,1,0:T(1,128)}), f32[512,1,256]{2,1,0:T(1,128)S(1)}, u32[]{:S(2)}, u32[]{:S(2)}) %all-to-all-start) | async-done | bytes 524320 | tf_op jit(solution)/shard_map/all_to_all | solution.py:15
  319.5 0.8 copy.11
  320.4 0.0 copy-done
  (31 shorter events, 0.4 us)
Async XLA Ops:
  7.2 35.9 %reduce-scatter.2.cloned.1.call-start = ((), (), s32[]{:S(2)}) async-start(), calls=%async_computation.2 | async-start | bytes 786432 | tf_op jit(solution)/shard_map/reduce_scatter | solution.py:31
  19.9 257.5 %all-reduce.3.cloned.1.call-start = ((), (), s32[]{:S(2)}) async-start(), calls=%async_computation.3 | async-start | bytes 524288
  280.6 38.9 %all-to-all-start = ((f32[512,1,256]{2,1,0:T(1,128)}), f32[512,1,256]{2,1,0:T(1,128)S(1)}, u32[]{:S(2)}, u32[]{:S(2)}) async-start(f32[512,1,256]{2,1,0:T(1,128)} %stack.2567), calls=%async_computation.1 | async-start | bytes 1048576 | tf_op jit(solution)/shard_map/all_to_all | solution.py:15
  300.4 20.0 %copy-start = (f32[131072]{0:T(1024)}, f32[131072]{0:T(1024)S(1)}, u32[]{:S(2)}) copy-start(f32[131072]{0:T(1024)S(1)} %scatter_fusion) | copy-start | bytes 1572868
Sparse Core Ops, SparseCore 0:
  20.0 22.9 reduce-scatter.1
  48.0 229.4 all-reduce.2
